TPU v7x, 32 devices: a whole 2x2x4 slice. The times are simulated.
32 devices in a mesh: ctx: 32 (over z, y, x, core), head: 1.
Axes of the slice: x: 2, y: 2, z: 4, core: 2. Of those that a mesh axis runs over, the one named last changes fastest.
Arguments:
- queries: bfloat16 [6144, 4096], P('ctx', 'head'), may hold values from -6 to 6
- keys: bfloat16 [6144, 1024], P('ctx', 'head'), may hold values from -6 to 6
- values: bfloat16 [6144, 1024], P('ctx', 'head'), may hold values from -6 to 6
- retrieval: int32 [32], replicated, may hold values 0 or 1
- spans: int32 [2, 32], replicated, may hold values from 64 to 4096, as said below
- out_weight: bfloat16 [4096, 4096], P(None, 'head'), may hold values from -0.09375 to 0.09375
Outputs:
- layer_out: bfloat16 [6144, 4096], P('ctx', 'head')
Inputs may be any that keep to these rules, and one draw needn't show every extreme that they name: `spans`: row 0 lies within 64 to 128, row 1 within 2048 to 4096; some head has exactly 128 sink tokens and some head exactly 4096 recent tokens.
All inputs are finite; a program needn't handle non-finite values.
Results may differ from a plain program's by a relative error of at most 0.0075.
Values may be sent and summed in bfloat16 or wider, within the bound.
A program may use at most 192 MiB of HBM per device.

v0:
```python
import jax
import jax.numpy as jnp
from jax import lax
from jax.sharding import PartitionSpec as P

HD = 128


def body(queries, keys, values, retrieval, spans, out_weight):
    row_count = queries.shape[0]
    half_rows = row_count // 2
    local_heads = queries.shape[1] // HD
    kv_heads = keys.shape[1] // HD
    group_size = local_heads // kv_heads
    scale = HD ** (-0.5)
    head_first = lax.axis_index("head") * local_heads
    retrieval_heads = (
        lax.dynamic_slice_in_dim(retrieval, head_first, local_heads).reshape(kv_heads, group_size)
        > 0
    )
    sink_sizes = lax.dynamic_slice_in_dim(spans[0], head_first, local_heads).reshape(
        kv_heads, group_size
    )
    window_sizes = lax.dynamic_slice_in_dim(spans[1], head_first, local_heads).reshape(
        kv_heads, group_size
    )
    cycle_index = lax.axis_index("ctx")
    near_queries = queries[:half_rows]
    far_queries = queries[half_rows:]
    near_pos = cycle_index * row_count + jnp.arange(half_rows, dtype=jnp.int32)
    far_pos = cycle_index * row_count + half_rows + jnp.arange(half_rows, dtype=jnp.int32)
    near_heads = near_queries.reshape(half_rows, kv_heads, group_size, HD)
    far_heads = far_queries.reshape(half_rows, kv_heads, group_size, HD)

    def update(state, query_heads, query_pos, key_heads, value_heads, key_pos):
        maxima, totals, accum = state
        scores = (
            jnp.einsum("qgjd,kgd->qgjk", query_heads, key_heads, preferred_element_type=jnp.float32)
            * scale
        )
        gap = query_pos[:, None] - key_pos[None, :]
        reach = retrieval_heads[None, :, :, None] | (
            key_pos[None, None, None, :] < sink_sizes[None, :, :, None]
        )
        reach = reach | (gap[:, None, None, :] < window_sizes[None, :, :, None])
        allowed = (gap >= 0)[:, None, None, :] & reach
        masked = jnp.where(allowed, scores, -1e30)
        fresh = jnp.maximum(maxima, jnp.max(masked, axis=-1))
        weights = jnp.where(allowed, jnp.exp(masked - fresh[..., None]), 0.0)
        totals = jnp.sum(weights, axis=-1)
        added = jnp.einsum(
            "qgjk,kgd->qgjd",
            weights.astype(jnp.bfloat16),
            value_heads,
            preferred_element_type=jnp.float32,
        )
        accum = added
        return (fresh, totals, accum)

    def visit(state, query_heads, query_pos, key_heads, value_heads, key_pos, offset):

        def active(held):
            return update(held, query_heads, query_pos, key_heads, value_heads, key_pos)

        def skipped(held):
            return held

        return lax.cond(offset <= query_pos[-1], active, skipped, state)

    start_state = (
        jnp.full((half_rows, kv_heads, group_size), -1e30, jnp.float32),
        jnp.zeros((half_rows, kv_heads, group_size), jnp.float32),
        jnp.zeros((half_rows, kv_heads, group_size, HD), jnp.float32),
    )
    pieces = (
        lax.all_gather(keys, "ctx", axis=0, tiled=True),
        lax.all_gather(values, "ctx", axis=0, tiled=True),
    )
    offset = jnp.int32(0)
    key_rows = pieces[0].shape[0]
    key_heads = pieces[0].reshape(key_rows, kv_heads, HD)
    value_heads = pieces[1].reshape(key_rows, kv_heads, HD)
    key_pos = jnp.arange(key_rows, dtype=jnp.int32)
    near_state = visit(start_state, near_heads, near_pos, key_heads, value_heads, key_pos, offset)
    far_state = visit(start_state, far_heads, far_pos, key_heads, value_heads, key_pos, offset)
    near_state, far_state = (near_state, far_state)

    def finish(state):
        return (
            (state[2] / state[1][..., None])
            .reshape(half_rows, local_heads * HD)
            .astype(jnp.bfloat16)
        )

    near_attended = finish(near_state)
    far_attended = finish(far_state)
    attended = jnp.concatenate([near_attended, far_attended], axis=0)
    features = lax.all_gather(attended, "head", axis=1, tiled=True)
    projected = jnp.dot(features, out_weight, preferred_element_type=jnp.float32)
    return projected.astype(jnp.bfloat16)


def solution(mesh):
    in_specs = (P("ctx", "head"), P("ctx", "head"), P("ctx", "head"), P(), P(), P(None, "head"))
    out_specs = P("ctx", "head")
    return jax.shard_map(body, mesh=mesh, in_specs=in_specs, out_specs=out_specs, check_vma=False)
```

profile of v0, /device:TPU:0, one launch (start us, length us, event | category | flops | bytes accessed | tf_op | source)
XLA Modules:
  0.0 474.7 jit_solution(1809647474993605472)
XLA Ops:
  6.5 0.0 all-gather.3.cloned.1.call-start
  6.5 0.7 all-gather.3.cloned.1.call-update
  7.3 0.0 all-gather.5.cloned.1.call-start
  7.3 0.7 all-gather.5.cloned.1.call-update
  8.0 0.6 slice.20
  9.3 0.0 copy-start.1
  9.3 0.6 slice.23
  10.5 0.0 copy-done.1
  10.5 0.7 broadcast_compare_fusion.2
  11.2 0.1 gt.11
  11.3 0.8 slice_bitcast_fusion
  12.0 96.1 %all-gather.3.cloned.1.call-done = bf16[6144,1024]{1,0:T(8,128)(2,1)} async-done(((bf16[192,1024]{1,0:T(8,128)(2,1)}), bf16[6144,1024]{1,0:T(8,128)(2,1)}) %all-gather.3.cloned.1.call-update) | async-done | bytes 12582928 | tf_op jit(solution)/shard_map/all_gather | solution.py:76
  108.1 16.8 %copy.23 = bf16[6144,1024]{0,1:T(8,128)(2,1)} copy(bf16[6144,1024]{1,0:T(8,128)(2,1)} %all-gather.3.cloned.1.call-done) | data formatting | bytes 25165824 | tf_op jit(solution)/shard_map/all_gather | solution.py:76
  124.9 0.0 copy-start
  124.9 79.9 %all-gather.5.cloned.1.call-done = bf16[6144,1024]{1,0:T(8,128)(2,1)} async-done(((bf16[192,1024]{1,0:T(8,128)(2,1)}), bf16[6144,1024]{1,0:T(8,128)(2,1)}) %all-gather.5.cloned.1.call-update) | async-done | bytes 12582928 | tf_op jit(solution)/shard_map/all_gather | solution.py:77
  204.8 16.7 %copy.24 = bf16[6144,1024]{0,1:T(8,128)(2,1)} copy(bf16[6144,1024]{1,0:T(8,128)(2,1)} %all-gather.5.cloned.1.call-done) | data formatting | bytes 25165824 | tf_op jit(solution)/shard_map/all_gather | solution.py:77
  221.5 0.0 copy-done
  221.5 0.0 copy-start.2
  221.5 111.5 %conditional.2 = (f32[96,8,4]{0,2,1:T(4,128)S(1)}, f32[96,8,4,128]{3,0,2,1:T(8,128)}) conditional(s32[]{:T(128)} %bitcast.8, () %tuple.21, (s32[96]{0:T(128)S(1)}, s32[6144]{0:T(1024)S(1)}, pred[8,4]{1,0:T(8,128)(4,1)S(1)}, s32[6144]{0:T(1024)S(1)}, s32[32]{0:T(128)S(1)}, /*index=5*/s32[32]{0:T(128)S(1)}, bf16[192,4096]{1,0:T(8,128)(2,1)S(1)}, ...), branch_computations={%region_0.0_spmd, %region_1.4_spmd} | conditional | flops 10081072128 | bytes 269895488 | solution.py:68
  221.5 0.1 lt.62
  221.6 0.1 lt.41
  221.7 0.3 compare_or_fusion
  222.0 0.4 broadcast_compare_fusion
  222.5 0.1 slice.14
  222.5 1.4 reshape.145
  224.0 0.3 broadcast_subtract_fusion
  224.2 34.7 %fusion = (f32[96,8,4]{0,2,1:T(4,128)S(1)}, f32[8,6144,96,4]{1,2,3,0:T(8,128)}) fusion(s32[8,4]{1,0:T(8,128)S(1)} %lt.62, s32[96,6144]{1,0:T(8,128)S(1)} %broadcast_subtract_fusion, pred[8,4,6144]{2,1,0:T(4,128)(4,1)S(1)} %compare_or_fusion, pred[96,6144]{1,0:T(8,128)(4,1)S(1)} %broadcast_compare_fusion, bf16[96,8,4,128]{3,2,1,0:T(4,128)(2,1)} %reshape.145, ...), kind=kOutput, calls=%fused_computation.3 | convolution fusion | flops 4945081344 | bytes 92024960 | tf_op jit(solution)/shard_map/cond/branch_1_fun/qgjd,kgd->qgjk/dot_general | solution.py:38
  259.0 35.2 %fusion.10 = f32[96,8,4,128]{3,0,2,1:T(8,128)} fusion(bf16[6144,8,128]{0,2,1:T(8,128)(2,1)} %get-tuple-element.95, f32[8,6144,96,4]{1,2,3,0:T(8,128)} %get-tuple-element.106, f32[96,8,4]{0,2,1:T(4,128)S(1)} %broadcast_maximum_fusion, s32[8,4]{1,0:T(8,128)S(1)} %lt.62, s32[96,6144]{1,0:T(8,128)S(1)} %broadcast_subtract_fusion, ...), kind=kOutput, calls=%fused_computation.12 | convolution fusion | flops 4982833152 | bytes 92811392 | tf_op jit(solution)/shard_map/cond/branch_1_fun/qgjk,kgd->qgjd/dot_general | solution.py:51
  294.2 38.6 %fusion.2 = f32[96,8,4]{0,2,1:T(4,128)S(1)} fusion(f32[8,6144,96,4]{1,2,3,0:T(8,128)} %get-tuple-element.106, f32[96,8,4]{0,2,1:T(4,128)S(1)} %broadcast_maximum_fusion, s32[8,4]{1,0:T(8,128)S(1)} %lt.62, s32[96,6144]{1,0:T(8,128)S(1)} %broadcast_subtract_fusion, pred[8,4,6144]{2,1,0:T(4,128)(4,1)S(1)} %compare_or_fusion, ...), kind=kLoop, calls=%fused_computation.5 | loop fusion | flops 150991872 | bytes 78667904 | tf_op jit(solution)/shard_map/cond/branch_1_fun/reduce_sum | solution.py:50
  333.0 1.9 divide_convert_fusion.1
  334.9 0.4 copy.27
  335.3 1.5 convert_element_type.36
  336.8 0.0 copy-done.2
  336.8 112.8 %conditional.3 = (f32[96,8,4]{0,2,1:T(4,128)S(1)}, f32[96,8,4,128]{3,0,2,1:T(8,128)}) conditional(s32[]{:T(128)} %bitcast.13, () %tuple.23, (s32[96]{0:T(128)S(1)}, s32[6144]{0:T(1024)S(1)}, pred[8,4]{1,0:T(8,128)(4,1)S(1)}, s32[6144]{0:T(1024)S(1)}, s32[32]{0:T(128)S(1)}, /*index=5*/s32[32]{0:T(128)S(1)}, bf16[192,4096]{1,0:T(8,128)(2,1)}, ...), branch_computations={%region_4.5_spmd, %region_5.8_spmd} | conditional | flops 10081072128 | bytes 269895488 | solution.py:68
  336.8 0.1 lt.70
  336.8 0.1 lt.66
  336.9 0.3 compare_or_fusion.1
  337.3 0.4 broadcast_compare_fusion.1
  337.7 1.2 slice.15
  338.9 1.4 reshape.146
  340.4 0.3 broadcast_subtract_fusion.1
  340.6 34.8 %fusion.19 = (f32[96,8,4]{0,2,1:T(4,128)S(1)}, f32[8,6144,96,4]{1,2,3,0:T(8,128)}) fusion(s32[8,4]{1,0:T(8,128)S(1)} %lt.70, s32[96,6144]{1,0:T(8,128)S(1)} %broadcast_subtract_fusion.1, pred[8,4,6144]{2,1,0:T(4,128)(4,1)S(1)} %compare_or_fusion.1, pred[96,6144]{1,0:T(8,128)(4,1)S(1)} %broadcast_compare_fusion.1, bf16[96,8,4,128]{3,2,1,0:T(4,128)(2,1)} %reshape.146, ...), kind=kOutput, calls=%fused_computation.24 | convolution fusion | flops 4945081344 | bytes 92024960 | tf_op jit(solution)/shard_map/cond/branch_1_fun/qgjd,kgd->qgjk/dot_general | solution.py:38
  375.4 35.2 %fusion.29 = f32[96,8,4,128]{3,0,2,1:T(8,128)} fusion(bf16[6144,8,128]{0,2,1:T(8,128)(2,1)} %get-tuple-element.104, f32[8,6144,96,4]{1,2,3,0:T(8,128)} %get-tuple-element.108, f32[96,8,4]{0,2,1:T(4,128)S(1)} %broadcast_maximum_fusion.1, s32[8,4]{1,0:T(8,128)S(1)} %lt.70, s32[96,6144]{1,0:T(8,128)S(1)} %broadcast_subtract_fusion.1, ...), kind=kOutput, calls=%fused_computation.33 | convolution fusion | flops 4982833152 | bytes 92811392 | tf_op jit(solution)/shard_map/cond/branch_1_fun/qgjk,kgd->qgjd/dot_general | solution.py:51
  410.7 38.6 %fusion.21 = f32[96,8,4]{0,2,1:T(4,128)S(1)} fusion(f32[8,6144,96,4]{1,2,3,0:T(8,128)} %get-tuple-element.108, f32[96,8,4]{0,2,1:T(4,128)S(1)} %broadcast_maximum_fusion.1, s32[8,4]{1,0:T(8,128)S(1)} %lt.70, s32[96,6144]{1,0:T(8,128)S(1)} %broadcast_subtract_fusion.1, pred[8,4,6144]{2,1,0:T(4,128)(4,1)S(1)} %compare_or_fusion.1, ...), kind=kLoop, calls=%fused_computation.26 | loop fusion | flops 150991872 | bytes 78667904 | tf_op jit(solution)/shard_map/cond/branch_1_fun/reduce_sum | solution.py:50
  449.5 1.9 divide_convert_fusion
  451.4 0.4 copy.30
  451.9 0.6 convert_element_type.40
  452.5 15.4 %convolution_convert_fusion = bf16[192,4096]{1,0:T(8,128)(2,1)} fusion(bf16[4096,4096]{1,0:T(8,128)(2,1)} %param.15, bf16[96,4096]{1,0:T(8,128)(2,1)S(1)} %convert_element_type.40, bf16[96,4096]{1,0:T(8,128)(2,1)} %convert_element_type.36), kind=kOutput, calls=%fused_computation.42 | convolution fusion | flops 6446383104 | bytes 36700160 | tf_op jit(solution)/shard_map/dot_general | solution.py:99
  (6 shorter events, 0.0 us)
Async XLA Ops:
  6.5 101.6 %all-gather.3.cloned.1.call-start = ((), (), s32[]{:S(2)}) async-start(), calls=%async_computation | async-start | bytes 12976128 | tf_op jit(solution)/shard_map/all_gather | solution.py:76
  7.3 197.5 %all-gather.5.cloned.1.call-start = ((), (), s32[]{:S(2)}) async-start(), calls=%async_computation.1 | async-start | bytes 12976128 | tf_op jit(solution)/shard_map/all_gather | solution.py:77
  9.3 1.2 copy-start.1
  124.9 96.6 %copy-start = (bf16[192,4096]{1,0:T(8,128)(2,1)S(1)}, bf16[192,4096]{1,0:T(8,128)(2,1)}, u32[]{:S(2)}) copy-start(bf16[192,4096]{1,0:T(8,128)(2,1)} %param.10) | copy-start | bytes 4718596
  221.5 115.3 %copy-start.2 = (s32[96]{0:T(128)S(1)}, s32[96]{0:T(128)}, u32[]{:S(2)}) copy-start(s32[96]{0:T(128)} %copy-done.1) | copy-start | bytes 1156
Sparse Core Ops, SparseCore 0:
  10.2 97.8 all-gather.2
  111.0 93.7 all-gather.4
where the time goes:
time: 476 us; the launch traced here: 475 us
  waiting for transfers between devices  177 us (37%)
  matrix products  155 us (33%)
  other arithmetic  83.7 us (18%)
  local copies, waits for them, and re-layouts  42.8 us (9%)
  between operations  14.8 us (3%)
    all_gather x1, waiting for transfers between devices, body(): lax.all_gather(keys, 'ctx', axis=0, tiled=True)  96.1 us
    all_gather x1, waiting for transfers between devices, body(): lax.all_gather(values, 'ctx', axis=0, tiled=True)  79.9 us
    reduce_sum x2, other arithmetic, update(): totals = jnp.sum(weights, axis=-1)  77.2 us
    dot_general x2, matrix products, update(): jnp.einsum('qgjk,kgd->qgjd', weights.astype(jnp.bfloat16), value_heads, p...  70.4 us
    dot_general x2, matrix products, update(): jnp.einsum('qgjd,kgd->qgjk', query_heads, key_heads, preferred_element_ty...  69.5 us
    all_gather x1, local copies, waits for them, and re-layouts, body(): lax.all_gather(keys, 'ctx', axis=0, tiled=True)  16.8 us
    all_gather x1, local copies, waits for them, and re-layouts, body(): lax.all_gather(values, 'ctx', axis=0, tiled=True)  16.7 us
    dot_general x1, matrix products, body(): jnp.dot(features, out_weight, preferred_element_type=jnp.float32)  15.4 us
  transfers between devices with their start and end apart: 2, of which 2 were waited for; matrix products, arithmetic and copies ran while one was open for 4% of the time, Pallas kernels for 0%

commit v1 on v0

--- a/solution.py
+++ b/solution.py
@@ -73,7 +73,9 @@
         jnp.zeros((half_rows, kv_heads, group_size, HD), jnp.float32),
     )
     pieces = (
-        lax.all_gather(keys, "ctx", axis=0, tiled=True),
+        jnp.concatenate(
+            lax.all_to_all(jnp.stack([keys] * lax.axis_size("ctx")), "ctx", 0, 0), axis=0
+        ),
         lax.all_gather(values, "ctx", axis=0, tiled=True),
     )
     offset = jnp.int32(0)

time: 476 us -> 649 us (1.36)
  waiting for transfers between devices: 177 us -> 333 us
  starting transfers between devices: 0.04 us -> 7.48 us
    all_to_all x0 -> x1, waiting for transfers between devices: none -> 332 us  [body(): lax.all_to_all(jnp.stack([keys] * lax.axis_size('ctx')), 'ctx', 0, 0)]
    all_gather x1 -> x0, waiting for transfers between devices: 96.1 us -> none  [body(): lax.all_gather(keys, 'ctx', axis=0, tiled=True)]
    all_gather x1, waiting for transfers between devices: 79.9 us -> 0.01 us  [body(): lax.all_gather(values, 'ctx', axis=0, tiled=True)]
    all_gather x1 -> x0, local copies, waits for them, and re-layouts: 16.8 us -> none  [body(): lax.all_gather(keys, 'ctx', axis=0, tiled=True)]
    unnamed x6 -> x7, local copies, waits for them, and re-layouts: 0.01 us -> 11.9 us
    all_to_all x0 -> x1, starting transfers between devices: none -> 7.44 us  [body(): lax.all_to_all(jnp.stack([keys] * lax.axis_size('ctx')), 'ctx', 0, 0)]
    another operation x0 -> x1, local copies, waits for them, and re-layouts: none -> 7.21 us  [body(): jnp.stack([keys] * lax.axis_size('ctx'))]
  transfers between devices with their start and end apart: 2 -> 2, of which waited for: 2 -> 1; matrix products, arithmetic and copies ran while one was open for 4% -> 2% of each run, Pallas kernels for 0% -> 0%
where the time goes in v1:
time: 649 us; the launch traced here: 644 us
  waiting for transfers between devices  333 us (51%)
  matrix products  161 us (25%)
  other arithmetic  83 us (13%)
  local copies, waits for them, and re-layouts  44.5 us (7%)
  between operations  15 us (2%)
  starting transfers between devices  7.48 us (1%)
    all_to_all x1, waiting for transfers between devices, body(): lax.all_to_all(jnp.stack([keys] * lax.axis_size('ctx')), 'ctx', 0, 0)  332 us
    reduce_sum x2, other arithmetic, update(): totals = jnp.sum(weights, axis=-1)  77.2 us
    dot_general x2, matrix products, update(): jnp.einsum('qgjd,kgd->qgjk', query_heads, key_heads, preferred_element_ty...  75.1 us
    dot_general x2, matrix products, update(): jnp.einsum('qgjk,kgd->qgjd', weights.astype(jnp.bfloat16), value_heads, p...  70.6 us
    all_gather x1, local copies, waits for them, and re-layouts, body(): lax.all_gather(values, 'ctx', axis=0, tiled=True)  16.8 us
    dot_general x1, matrix products, body(): jnp.dot(features, out_weight, preferred_element_type=jnp.float32)  15.4 us
  transfers between devices with their start and end apart: 2, of which 1 were waited for; matrix products, arithmetic and copies ran while one was open for 2% of the time, Pallas kernels for 0%

profile of v1, /device:TPU:0, one launch (start us, length us, event | category | flops | bytes accessed | tf_op | source)
XLA Modules:
  0.0 644.5 jit_solution(3252595035577842336)
XLA Ops:
  6.5 0.0 copy-start.2
  6.5 0.0 copy-start.1
  6.5 7.2 %stack.2 = bf16[32,192,1024]{2,1,0:T(8,128)(2,1)} broadcast(bf16[192,1024]{1,0:T(8,128)(2,1)} %param.11), dimensions={1,2} | broadcast | bytes 12976128 | tf_op jit(solution)/shard_map/stack | solution.py:77
  13.8 7.4 %all-to-all-start = ((bf16[32,192,1024]{2,1,0:T(8,128)(2,1)}), bf16[32,192,1024]{2,1,0:T(8,128)(2,1)}, u32[]{:S(2)}, u32[]{:S(2)}) async-start(bf16[32,192,1024]{2,1,0:T(8,128)(2,1)} %stack.2), calls=%async_computation | async-start | bytes 25165824 | tf_op jit(solution)/shard_map/all_to_all | solution.py:77
  21.2 0.0 all-gather.2.cloned.1.call-start
  21.2 0.7 all-gather.2.cloned.1.call-update
  22.0 0.6 slice.20
  23.2 0.6 slice.23
  24.4 0.0 copy-done.2
  24.5 0.1 gt.11
  24.5 0.0 copy-done.1
  24.6 331.9 %all-to-all-done = bf16[32,192,1024]{2,1,0:T(8,128)(2,1)} async-done(((bf16[32,192,1024]{2,1,0:T(8,128)(2,1)}), bf16[32,192,1024]{2,1,0:T(8,128)(2,1)}, u32[]{:S(2)}, u32[]{:S(2)}) %all-to-all-start) | async-done | bytes 12582944 | tf_op jit(solution)/shard_map/all_to_all | solution.py:77
  356.4 11.9 %copy.41 = bf16[768,8,8,128]{3,2,1,0:T(8,128)(2,1)} copy(bf16[768,8,8,128]{3,1,2,0:T(8,128)(2,1)} %bitcast.18) | data formatting | bytes 25165824
  368.3 0.0 copy-start
  368.3 0.0 all-gather.2.cloned.1.call-done
  368.3 16.8 %copy.22 = bf16[6144,1024]{0,1:T(8,128)(2,1)} copy(bf16[6144,1024]{1,0:T(8,128)(2,1)} %all-gather.2.cloned.1.call-done) | data formatting | bytes 25165824 | tf_op jit(solution)/shard_map/all_gather | solution.py:79
  385.1 0.0 copy-done
  385.1 114.0 %conditional.2 = (f32[96,8,4]{0,2,1:T(4,128)S(1)}, f32[96,8,4,128]{3,0,2,1:T(8,128)}) conditional(s32[]{:T(128)} %bitcast.8, () %tuple.21, (s32[96]{0:T(128)S(1)}, s32[6144]{0:T(1024)S(1)}, pred[8,4]{1,0:T(8,128)(4,1)S(1)}, s32[6144]{0:T(1024)S(1)}, s32[32]{0:T(128)S(1)}, /*index=5*/s32[32]{0:T(128)S(1)}, bf16[192,4096]{1,0:T(8,128)(2,1)S(1)}, ...), branch_computations={%region_0.0_spmd, %region_1.4_spmd} | conditional | flops 10081072128 | bytes 269895488 | solution.py:68
  385.2 0.1 lt.62
  385.2 0.1 lt.41
  385.3 0.3 compare_or_fusion
  385.7 0.4 broadcast_compare_fusion
  386.1 0.1 slice.14
  386.2 1.4 reshape.145
  387.6 0.3 broadcast_subtract_fusion
  387.9 36.9 %fusion = (f32[96,8,4]{0,2,1:T(4,128)S(1)}, f32[8,6144,96,4]{1,2,3,0:T(8,128)}) fusion(s32[8,4]{1,0:T(8,128)S(1)} %lt.62, s32[96,6144]{1,0:T(8,128)S(1)} %broadcast_subtract_fusion, pred[8,4,6144]{2,1,0:T(4,128)(4,1)S(1)} %compare_or_fusion, pred[96,6144]{1,0:T(8,128)(4,1)S(1)} %broadcast_compare_fusion, bf16[96,8,4,128]{3,2,1,0:T(4,128)(2,1)} %reshape.145, ...), kind=kOutput, calls=%fused_computation.3 | convolution fusion | flops 4945081344 | bytes 92024960 | tf_op jit(solution)/shard_map/cond/branch_1_fun/qgjd,kgd->qgjk/dot_general | solution.py:38
  424.8 35.3 %fusion.10 = f32[96,8,4,128]{3,0,2,1:T(8,128)} fusion(bf16[6144,8,128]{0,2,1:T(8,128)(2,1)} %get-tuple-element.95, f32[8,6144,96,4]{1,2,3,0:T(8,128)} %get-tuple-element.106, f32[96,8,4]{0,2,1:T(4,128)S(1)} %broadcast_maximum_fusion, s32[8,4]{1,0:T(8,128)S(1)} %lt.62, s32[96,6144]{1,0:T(8,128)S(1)} %broadcast_subtract_fusion, ...), kind=kOutput, calls=%fused_computation.12 | convolution fusion | flops 4982833152 | bytes 92811392 | tf_op jit(solution)/shard_map/cond/branch_1_fun/qgjk,kgd->qgjd/dot_general | solution.py:51
  460.1 38.6 %fusion.2 = f32[96,8,4]{0,2,1:T(4,128)S(1)} fusion(f32[8,6144,96,4]{1,2,3,0:T(8,128)} %get-tuple-element.106, f32[96,8,4]{0,2,1:T(4,128)S(1)} %broadcast_maximum_fusion, s32[8,4]{1,0:T(8,128)S(1)} %lt.62, s32[96,6144]{1,0:T(8,128)S(1)} %broadcast_subtract_fusion, pred[8,4,6144]{2,1,0:T(4,128)(4,1)S(1)} %compare_or_fusion, ...), kind=kLoop, calls=%fused_computation.5 | loop fusion | flops 150991872 | bytes 78667904 | tf_op jit(solution)/shard_map/cond/branch_1_fun/reduce_sum | solution.py:50
  499.2 1.9 divide_convert_fusion.1
  501.1 0.4 copy.25
  501.5 1.5 convert_element_type.36
  503.0 116.2 %conditional.3 = (f32[96,8,4]{0,2,1:T(4,128)S(1)}, f32[96,8,4,128]{3,0,2,1:T(8,128)}) conditional(s32[]{:T(128)} %bitcast.12, () %tuple.23, (s32[96]{0:T(128)S(1)}, s32[6144]{0:T(1024)S(1)}, pred[8,4]{1,0:T(8,128)(4,1)S(1)}, s32[6144]{0:T(1024)S(1)}, s32[32]{0:T(128)S(1)}, /*index=5*/s32[32]{0:T(128)S(1)}, bf16[192,4096]{1,0:T(8,128)(2,1)}, ...), branch_computations={%region_4.5_spmd, %region_5.8_spmd} | conditional | flops 10081072128 | bytes 269895488 | solution.py:68
  503.0 0.1 lt.70
  503.1 0.1 lt.66
  503.1 0.3 compare_or_fusion.1
  503.5 0.4 broadcast_compare_fusion.1
  503.9 1.2 slice.15
  505.1 1.4 reshape.146
  506.6 0.3 broadcast_subtract_fusion.1
  506.8 38.2 %fusion.19 = (f32[96,8,4]{0,2,1:T(4,128)S(1)}, f32[8,6144,96,4]{1,2,3,0:T(8,128)}) fusion(s32[8,4]{1,0:T(8,128)S(1)} %lt.70, s32[96,6144]{1,0:T(8,128)S(1)} %broadcast_subtract_fusion.1, pred[8,4,6144]{2,1,0:T(4,128)(4,1)S(1)} %compare_or_fusion.1, pred[96,6144]{1,0:T(8,128)(4,1)S(1)} %broadcast_compare_fusion.1, bf16[96,8,4,128]{3,2,1,0:T(4,128)(2,1)} %reshape.146, ...), kind=kOutput, calls=%fused_computation.24 | convolution fusion | flops 4945081344 | bytes 92024960 | tf_op jit(solution)/shard_map/cond/branch_1_fun/qgjd,kgd->qgjk/dot_general | solution.py:38
  545.1 35.3 %fusion.29 = f32[96,8,4,128]{3,0,2,1:T(8,128)} fusion(bf16[6144,8,128]{0,2,1:T(8,128)(2,1)} %get-tuple-element.104, f32[8,6144,96,4]{1,2,3,0:T(8,128)} %get-tuple-element.108, f32[96,8,4]{0,2,1:T(4,128)S(1)} %broadcast_maximum_fusion.1, s32[8,4]{1,0:T(8,128)S(1)} %lt.70, s32[96,6144]{1,0:T(8,128)S(1)} %broadcast_subtract_fusion.1, ...), kind=kOutput, calls=%fused_computation.33 | convolution fusion | flops 4982833152 | bytes 92811392 | tf_op jit(solution)/shard_map/cond/branch_1_fun/qgjk,kgd->qgjd/dot_general | solution.py:51
  580.3 38.6 %fusion.21 = f32[96,8,4]{0,2,1:T(4,128)S(1)} fusion(f32[8,6144,96,4]{1,2,3,0:T(8,128)} %get-tuple-element.108, f32[96,8,4]{0,2,1:T(4,128)S(1)} %broadcast_maximum_fusion.1, s32[8,4]{1,0:T(8,128)S(1)} %lt.70, s32[96,6144]{1,0:T(8,128)S(1)} %broadcast_subtract_fusion.1, pred[8,4,6144]{2,1,0:T(4,128)(4,1)S(1)} %compare_or_fusion.1, ...), kind=kLoop, calls=%fused_computation.26 | loop fusion | flops 150991872 | bytes 78667904 | tf_op jit(solution)/shard_map/cond/branch_1_fun/reduce_sum | solution.py:50
  619.1 1.9 divide_convert_fusion
  621.0 0.4 copy.28
  621.5 0.6 convert_element_type.40
  622.1 15.4 %convolution_convert_fusion = bf16[192,4096]{1,0:T(8,128)(2,1)} fusion(bf16[4096,4096]{1,0:T(8,128)(2,1)} %param.15, bf16[96,4096]{1,0:T(8,128)(2,1)S(1)} %convert_element_type.40, bf16[96,4096]{1,0:T(8,128)(2,1)} %convert_element_type.36), kind=kOutput, calls=%fused_computation.42 | convolution fusion | flops 6446383104 | bytes 36700160 | tf_op jit(solution)/shard_map/dot_general | solution.py:101
  (8 shorter events, 0.0 us)
Async XLA Ops:
  6.5 17.9 %copy-start.2 = (s32[32]{0:T(128)S(1)}, s32[32]{0:T(128)}, u32[]{:S(2)}) copy-start(s32[32]{0:T(128)} %param.13) | copy-start | bytes 388
  6.5 18.0 %copy-start.1 = (s32[2,32]{1,0:T(2,128)S(1)}, s32[2,32]{1,0:T(2,128)}, u32[]{:S(2)}) copy-start(s32[2,32]{1,0:T(2,128)} %param.14) | copy-start | bytes 772
  13.8 342.7 %all-to-all-start = ((bf16[32,192,1024]{2,1,0:T(8,128)(2,1)}), bf16[32,192,1024]{2,1,0:T(8,128)(2,1)}, u32[]{:S(2)}, u32[]{:S(2)}) async-start(bf16[32,192,1024]{2,1,0:T(8,128)(2,1)} %stack.2), calls=%async_computation | async-start | bytes 25165824 | tf_op jit(solution)/shard_map/all_to_all | solution.py:77
  21.2 347.1 %all-gather.2.cloned.1.call-start = ((), (), s32[]{:S(2)}) async-start(), calls=%async_computation.1 | async-start | bytes 12976128 | tf_op jit(solution)/shard_map/all_gather | solution.py:79
  368.3 16.8 %copy-start = (bf16[192,4096]{1,0:T(8,128)(2,1)S(1)}, bf16[192,4096]{1,0:T(8,128)(2,1)}, u32[]{:S(2)}) copy-start(bf16[192,4096]{1,0:T(8,128)(2,1)} %param.10) | copy-start | bytes 4718596
Sparse Core Ops, SparseCore 0:
  24.9 217.5 all-gather.1
